TPU v7x, 128 devices: a whole 4x4x4 slice. The times are simulated.
128 devices in a mesh: ctx: 16 (over x, z_hi, core), exp: 8 (over y, z_lo).
Axes of the slice: x: 4, y: 4, z: 4 (z_hi: 2, z_lo: 2; z = z_hi * 2 + z_lo), core: 2. Of those that a mesh axis runs over, the one named last changes fastest.
Arguments:
- query: bfloat16 [2048, 4096], P('ctx', 'exp'), may hold values from -8 to 8
- keys_values: bfloat16 [2, 2048, 1024], P(None, 'ctx', 'exp'), may hold values from -8 to 8
- cache: bfloat16 [2, 4096, 1024], P(None, 'ctx', 'exp'), may hold values from -8 to 8
- residual: bfloat16 [2048, 4096], P(('ctx', 'exp')), may hold values from -6 to 6
- out_proj: bfloat16 [4096, 4096], P('exp'), may hold values from -0.09375 to 0.09375
- norm_gain: float32 [4096], replicated, may hold values from 0.1 to 1.9
- router: bfloat16 [4096, 8], replicated, may hold values from -0.09375 to 0.09375
- expert_ids: int32 [2048, 2], P(('ctx', 'exp')), may hold values from 0 to 7, all different within a row; in each aligned block of 16 rows (0 to 15, 16 to 31, ...) at most 8 rows name the same one
- w_gate: bfloat16 [8, 4096, 8192], P('exp', None, 'ctx'), may hold values from -0.09375 to 0.09375
- w_up: bfloat16 [8, 4096, 8192], P('exp', None, 'ctx'), may hold values from -0.09375 to 0.09375
- w_down: bfloat16 [8, 8192, 4096], P('exp', 'ctx'), may hold values from -0.0625 to 0.0625
- cotangent: bfloat16 [2048, 4096], P(('ctx', 'exp')), may hold values from -6 to 6
Outputs:
- layer_out: bfloat16 [2048, 4096], P(('ctx', 'exp'))
- grad_down: float32 [8, 8192, 4096], P('exp', 'ctx')
Inputs may be any that keep to these rules, and one draw needn't show every extreme that they name: `expert_ids`: each row names two different experts. Within each aligned block of 16 rows no expert is named by more than 8 rows.
All inputs are finite; a program needn't handle non-finite values.
Results may differ from a plain program's by a relative error of at most 0.012.
Values may be sent and summed in bfloat16 or wider, within the bound.
A program may use at most 128 MiB of HBM per device.

v0:
```python
import math

import jax
import jax.numpy as jnp
from jax import lax
from jax.sharding import PartitionSpec as P

QUERY_HEADS = 32
KEY_VALUE_HEADS = 8
HEAD_SIZE = 128
WINDOW = 4096


epsilon = 1e-05


def from_behind(shard, axis, by):
    devices = lax.axis_size(axis)
    return lax.ppermute(shard, axis, [(i, (i + by) % devices) for i in range(devices)])


def in_blocks(shard, dim, devices):
    before, after = (shard.shape[:dim], shard.shape[dim + 1 :])
    return jnp.moveaxis(shard.reshape(*before, devices, -1, *after), dim, 0)


def summed_on_arrival(shard, axis, dim):
    blocks = in_blocks(shard, dim, lax.axis_size(axis))
    arrived = lax.all_to_all(blocks, axis, split_axis=0, concat_axis=0, tiled=True)
    return arrived.sum(axis=0)


def sent_together(arrays, axis, split_dim, concat_dim, along):
    both = jnp.concatenate(arrays, axis=along)
    whole, at, gathered = (
        lax.all_to_all(both, axis, split_axis=split_dim, concat_axis=concat_dim, tiled=True),
        0,
        [],
    )
    for a in arrays:
        gathered.append(lax.slice_in_dim(whole, at, at + a.shape[along], axis=along))
        at += a.shape[along]
    return tuple(gathered)


def in_one_piece(arrays, axis, dim, along):
    both = jnp.concatenate(arrays, axis=along)
    whole, at, gathered = (lax.all_gather(both, axis, axis=dim, tiled=True), 0, [])
    for a in arrays:
        gathered.append(lax.slice_in_dim(whole, at, at + a.shape[along], axis=along))
        at += a.shape[along]
    return tuple(gathered)


def attend_block(state, queries, kv_block, key_pos, query_pos):
    running_max, running_sum, numerator = state
    heads_kv = queries.shape[1]
    key_count = kv_block.shape[1]
    key_rows = kv_block[0].reshape(key_count, heads_kv, HEAD_SIZE)
    value_rows = kv_block[1].reshape(key_count, heads_kv, HEAD_SIZE)
    scores = jnp.einsum("thjd,khd->thjk", queries, key_rows, preferred_element_type=jnp.float32) * (
        1.0 / math.sqrt(HEAD_SIZE)
    )
    visible = (key_pos[None, :] <= query_pos[:, None]) & (
        key_pos[None, :] > query_pos[:, None] - WINDOW
    )
    visible = visible[:, None, None, :]
    scores = jnp.where(visible, scores, -1e30)
    new_max = jnp.maximum(running_max, jnp.max(scores, axis=-1))
    rescale = jnp.exp(running_max - new_max)
    weights = jnp.where(visible, jnp.exp(scores - new_max[..., None]), 0.0)
    running_sum = running_sum * rescale + jnp.sum(weights, axis=-1)
    numerator = numerator * rescale[..., None] + jnp.einsum(
        "thjk,khd->thjd",
        weights.astype(jnp.bfloat16),
        value_rows,
        preferred_element_type=jnp.float32,
    )
    return (new_max, running_sum, numerator)


def on_device(
    query,
    keys_values,
    cache,
    residual,
    out_proj,
    norm_gain,
    router,
    expert_ids,
    w_gate,
    w_up,
    w_down,
    cotangent,
):
    ctx_size = lax.axis_size("ctx")
    ctx_index = lax.axis_index("ctx")
    exp_size = lax.axis_size("exp")
    token_count = query.shape[0]
    prior_count = cache.shape[1]
    heads_kv = keys_values.shape[2] // HEAD_SIZE
    head_groups = QUERY_HEADS // KEY_VALUE_HEADS
    queries = query.reshape(token_count, heads_kv, head_groups, HEAD_SIZE)
    local_pos = jnp.arange(token_count, dtype=jnp.int32)
    cache_local = jnp.arange(prior_count, dtype=jnp.int32)
    query_pos = prior_count * ctx_size + ctx_index * token_count + local_pos

    def positions(slab_owner, cache_owner):
        return jnp.concatenate(
            [
                cache_owner * prior_count + cache_local,
                prior_count * ctx_size + slab_owner * token_count + local_pos,
            ]
        )

    start_state = (
        jnp.full((token_count, heads_kv, head_groups), -1e30, jnp.float32),
        jnp.zeros((token_count, heads_kv, head_groups), jnp.float32),
        jnp.zeros((token_count, heads_kv, head_groups, HEAD_SIZE), jnp.float32),
    )
    state = attend_block(
        start_state,
        queries,
        jnp.concatenate([cache, keys_values], axis=1),
        positions(ctx_index, ctx_index),
        query_pos,
    )

    def cycle_step(step, loop_state):
        inner, slab_block, cache_block = loop_state
        slab_block = from_behind(slab_block, "ctx", 1)
        cache_block = from_behind(cache_block, "ctx", -1)
        slab_owner = (ctx_index - step) % ctx_size
        cache_owner = (ctx_index + step) % ctx_size
        inner = attend_block(
            inner,
            queries,
            jnp.concatenate([cache_block, slab_block], axis=1),
            positions(slab_owner, cache_owner),
            query_pos,
        )
        return (inner, slab_block, cache_block)

    cycle_out = lax.fori_loop(1, ctx_size, cycle_step, (state, keys_values, cache))
    running_max, running_sum, numerator = cycle_out[0]
    attn = (
        (numerator / running_sum[..., None])
        .astype(jnp.bfloat16)
        .reshape(token_count, heads_kv * head_groups * HEAD_SIZE)
    )
    row_count = token_count // exp_size
    projected = summed_on_arrival(
        jnp.dot(attn, out_proj, preferred_element_type=jnp.float32), "exp", 0
    )
    hidden_one = residual.astype(jnp.float32) + projected
    mean_square = jnp.mean(hidden_one * hidden_one, axis=-1, keepdims=True)
    normed = (hidden_one * lax.rsqrt(mean_square + epsilon) * norm_gain).astype(jnp.bfloat16)
    logits = jnp.dot(normed, router, preferred_element_type=jnp.float32)
    experts = router.shape[1]
    onehot = (expert_ids[:, :, None] == jnp.arange(experts, dtype=jnp.int32)[None, None, :]).astype(
        jnp.float32
    )
    chosen = jnp.sum(onehot * logits[:, None, :], axis=-1)
    first = 1.0 / (1.0 + jnp.exp(chosen[:, 1] - chosen[:, 0]))
    gates = jnp.stack([first, 1.0 - first], axis=1)
    capacity = 4 * token_count // (exp_size * exp_size)
    assigned = row_count * 2
    flat_hot = onehot.reshape(assigned, experts)
    earlier = (jnp.arange(assigned)[:, None] > jnp.arange(assigned)[None, :]).astype(jnp.float32)
    before = jnp.dot(earlier, flat_hot)
    slot = jnp.sum(before * flat_hot, axis=-1).astype(jnp.int32)
    target = expert_ids.reshape(assigned) * capacity + slot
    dispatch = (jnp.arange(experts * capacity, dtype=jnp.int32)[:, None] == target[None, :]).astype(
        jnp.float32
    )
    dispatch = dispatch.reshape(experts * capacity, row_count, 2)
    pick_rows = jnp.sum(dispatch, axis=-1)
    weighted_rows = jnp.sum(dispatch * gates[None, :, :], axis=-1)
    outgoing = jnp.dot(
        pick_rows.astype(jnp.bfloat16), normed, preferred_element_type=jnp.float32
    ).astype(jnp.bfloat16)
    outgoing = outgoing.reshape(experts, capacity, normed.shape[1])
    scaled_grad = jnp.dot(weighted_rows, cotangent.astype(jnp.float32)).astype(jnp.bfloat16)
    scaled_grad = scaled_grad.reshape(experts, capacity, normed.shape[1])
    local_count = experts * capacity
    gate_mat = w_gate[0]
    up_mat = w_up[0]
    down_mat = w_down[0]
    arrived, arrived_grad = sent_together((outgoing, scaled_grad), "exp", 0, 0, 1)
    rows_all, grads_all = in_one_piece(
        (
            arrived.reshape(local_count, normed.shape[1]),
            arrived_grad.reshape(local_count, normed.shape[1]),
        ),
        "ctx",
        0,
        1,
    )
    gate_val = jnp.dot(rows_all, gate_mat, preferred_element_type=jnp.float32)
    up_val = jnp.dot(rows_all, up_mat, preferred_element_type=jnp.float32)
    hidden_all = (jax.nn.silu(gate_val) * up_val).astype(jnp.bfloat16)
    expert_out = lax.psum_scatter(
        jnp.dot(hidden_all, down_mat, preferred_element_type=jnp.float32).astype(jnp.bfloat16),
        "ctx",
        scatter_dimension=0,
        tiled=True,
    )
    returned = lax.all_to_all(
        expert_out.reshape(experts, capacity, normed.shape[1]),
        "exp",
        split_axis=0,
        concat_axis=0,
        tiled=True,
    )
    combined = jnp.dot(
        weighted_rows.T, returned.reshape(local_count, normed.shape[1]).astype(jnp.float32)
    )
    layer_out = (hidden_one + combined).astype(jnp.bfloat16)
    gradient = lax.dot_general(
        hidden_all, grads_all, (((0,), (0,)), ((), ())), preferred_element_type=jnp.float32
    )
    return (layer_out, gradient[None])


def solution(mesh):
    placed = (
        P("ctx", "exp"),
        P(None, "ctx", "exp"),
        P(None, "ctx", "exp"),
        P(("ctx", "exp"), None),
        P("exp", None),
        P(),
        P(),
        P(("ctx", "exp"), None),
        P("exp", None, "ctx"),
        P("exp", None, "ctx"),
        P("exp", "ctx", None),
        P(("ctx", "exp"), None),
    )
    return jax.shard_map(
        on_device,
        mesh=mesh,
        in_specs=placed,
        out_specs=(P(("ctx", "exp"), None), P("exp", "ctx", None)),
        check_vma=False,
    )
```

profile of v0, /device:TPU:26, one launch (start us, length us, event | category | flops | bytes accessed | tf_op | source)
XLA Modules:
  0.0 459.5 jit_solution(11231022430674638139)
XLA Ops:
  12.0 117.6 %while.24 = (s32[]{:T(128)}, f32[128,1,4]{0,2,1:T(4,128)S(1)}, f32[128,1,4]{0,2,1:T(4,128)S(1)}, f32[128,1,4,128]{0,3,2,1:T(8,128)S(1)}, bf16[2,128,128]{2,1,0:T...) while((s32[]{:T(128)}, f32[128,1,4]{0,2,1:T(4,128)S(1)}, ...), condition=%wide.region_5.6_spmd.clone, body=%wide.region_2.5_spmd.clone.sunk | while | flops 102713888 | bytes 5022215 | solution.py:144
  12.1 4.1 collective-permute-start
  16.4 1.8 collective-permute-done.1
  19.6 3.3 collective-permute-start.1
  27.5 2.4 collective-permute-start.1
  29.9 2.0 collective-permute-start
  36.8 2.9 collective-permute-start
  43.8 3.8 collective-permute-start
  51.7 3.8 collective-permute-start
  55.6 1.7 collective-permute-done.1
  59.5 3.8 collective-permute-start
  63.4 1.7 collective-permute-done.1
  67.4 3.8 collective-permute-start
  75.2 3.8 collective-permute-start
  83.1 3.8 collective-permute-start
  90.9 3.8 collective-permute-start
  98.8 3.9 collective-permute-start
  102.8 1.7 collective-permute-done.1
  106.7 3.8 collective-permute-start
  115.6 2.7 collective-permute-start
  121.8 2.9 collective-permute-start.1
  129.9 4.3 fusion.34
  134.2 6.2 %all-to-all-start = ((f32[8,16,4096]{2,1,0:T(8,128)}), f32[8,16,4096]{2,1,0:T(8,128)S(1)}, u32[]{:S(2)}, u32[]{:S(2)}) async-start(f32[8,16,4096]{2,1,0:T(8,128)} %fusion.34), calls=%async_computation | async-start | bytes 4194304 | tf_op jit(solution)/shard_map/all_to_all | solution.py:29
  140.8 25.2 %all-to-all-done = f32[8,16,4096]{2,1,0:T(8,128)S(1)} async-done(((f32[8,16,4096]{2,1,0:T(8,128)}), f32[8,16,4096]{2,1,0:T(8,128)S(1)}, u32[]{:S(2)}, u32[]{:S(2)}) %all-to-all-start) | async-done | bytes 2097184 | tf_op jit(solution)/shard_map/all_to_all | solution.py:29
  167.5 20.4 %all_to_all.15 = bf16[8,16,4096]{2,1,0:T(8,128)(2,1)S(1)} all-to-all(bf16[8,16,4096]{2,1,0:T(8,128)(2,1)S(1)} %pad_maximum_fusion), channel_id=1, replica_groups=mesh['ctx'=16,'exp'=8] {'exp'}, dimensions={0} | all-to-all | bytes 2097152 | tf_op jit(solution)/shard_map/all_to_all | solution.py:36
  189.1 121.9 %all-gather.2.cloned.1.call-done = bf16[1024,8192]{1,0:T(8,128)(2,1)} async-done(((bf16[64,8192]{1,0:T(8,128)(2,1)}), bf16[1024,8192]{1,0:T(8,128)(2,1)}) %all-gather.2.cloned.1.call-update) | async-done | bytes 16777232 | tf_op jit(solution)/shard_map/all_gather | solution.py:48
  311.1 10.5 %fusion.23 = f32[1024,512]{1,0:T(8,128)} fusion(bf16[1024,8192]{1,0:T(8,128)(2,1)} %all-gather.2.cloned.1.call-done, bf16[1,4096,512]{2,1,0:T(8,128)(2,1)} %param.22), kind=kOutput, calls=%fused_computation.36 | convolution fusion | flops 4294967296 | bytes 14680064 | tf_op jit(solution)/shard_map/dot_general | solution.py:199
  322.4 6.2 %multiply_convert_fusion = bf16[1024,512]{1,0:T(8,128)(2,1)S(1)} fusion(f32[1024,512]{1,0:T(8,128)} %fusion.23, bf16[1,4096,512]{2,1,0:T(8,128)(2,1)S(1)} %copy-done.7, bf16[1024,8192]{1,0:T(8,128)(2,1)S(1)} %copy-done.2), kind=kOutput, calls=%fused_computation.50 | convolution fusion | flops 4298113024 | bytes 15728640 | tf_op jit(solution)/shard_map/dot_general | solution.py:200
  328.6 6.8 %convolution_convert_fusion = bf16[1024,4096]{1,0:T(8,128)(2,1)} fusion(bf16[1024,512]{1,0:T(8,128)(2,1)S(1)} %multiply_convert_fusion, bf16[1,512,4096]{2,1,0:T(8,128)(2,1)S(1)} %copy-done.8), kind=kOutput, calls=%fused_computation.33 | convolution fusion | flops 4299161600 | bytes 13631488 | tf_op jit(solution)/shard_map/dot_general | solution.py:203
  335.4 101.3 %reduce-scatter.2.cloned.1.call-done = bf16[64,4096]{1,0:T(8,128)(2,1)} async-done(((bf16[1024,4096]{1,0:T(8,128)(2,1)}), bf16[64,4096]{1,0:T(8,128)(2,1)}) %reduce-scatter.2.cloned.1.call-update) | async-done | bytes 524304 | tf_op jit(solution)/shard_map/reduce_scatter | solution.py:202
  436.7 4.9 %all-to-all-start.2 = ((bf16[8,8,4096]{2,1,0:T(8,128)(2,1)}), bf16[8,8,4096]{2,1,0:T(8,128)(2,1)S(1)}, u32[]{:S(2)}, u32[]{:S(2)}) async-start(bf16[8,8,4096]{2,1,0:T(8,128)(2,1)} %bitcast.141), calls=%async_computation.3 | async-start | bytes 1048576 | tf_op jit(solution)/shard_map/all_to_all | solution.py:208
  441.6 10.2 %fusion.25 = f32[1,512,4096]{2,1,0:T(8,128)} fusion(bf16[1024,512]{1,0:T(8,128)(2,1)S(1)} %multiply_convert_fusion, bf16[1024,8192]{1,0:T(8,128)(2,1)} %all-gather.2.cloned.1.call-done), kind=kOutput, calls=%fused_computation.38 | convolution fusion | flops 4294967296 | bytes 17825792 | tf_op jit(solution)/shard_map/dot_general | solution.py:219
  (328 shorter events, 64.8 us)
Async XLA Ops:
  12.0 6.2 %collective-permute-start.1 = (bf16[2,128,128]{2,1,0:T(8,128)(2,1)S(1)}, bf16[2,128,128]{2,1,0:T(8,128)(2,1)S(1)}, u32[]{:S(2)}, u32[]{:S(2)}) collective-permute-start(bf16[2,128,128]{2,1,0:T(8,128)(2,1)S(1)} %get-tuple-element.454), channel_id=1, source_target_pairs={{0,8},{8,16},{16,24},{24,32},{32,40},{40,48},{48,56},{56,64},{64,7... | collective-permute-start | bytes 196616 | tf_op jit(solution)/shard_map/while/body/eval_jaxpr/ppermute | solution.py:19
  12.1 6.7 %collective-permute-start = (bf16[2,256,128]{2,1,0:T(8,128)(2,1)S(1)}, bf16[2,256,128]{2,1,0:T(8,128)(2,1)S(1)}, u32[]{:S(2)}, u32[]{:S(2)}) collective-permute-start(bf16[2,256,128]{2,1,0:T(8,128)(2,1)S(1)} %get-tuple-element.455), channel_id=1, source_target_pairs={{0,120},{8,0},{16,8},{24,16},{32,24},{40,32},{48,40},{56,48},{64,5... | collective-permute-start | bytes 393224 | tf_op jit(solution)/shard_map/while/body/eval_jaxpr/ppermute | solution.py:19
  19.6 6.3 %collective-permute-start.1 = (bf16[2,128,128]{2,1,0:T(8,128)(2,1)S(1)}, bf16[2,128,128]{2,1,0:T(8,128)(2,1)S(1)}, u32[]{:S(2)}, u32[]{:S(2)}) collective-permute-start(bf16[2,128,128]{2,1,0:T(8,128)(2,1)S(1)} %get-tuple-element.454), channel_id=1, source_target_pairs={{0,8},{8,16},{16,24},{24,32},{32,40},{40,48},{48,56},{56,64},{64,7... | collective-permute-start | bytes 196616 | tf_op jit(solution)/shard_map/while/body/eval_jaxpr/ppermute | solution.py:19
  27.5 6.3 %collective-permute-start.1 = (bf16[2,128,128]{2,1,0:T(8,128)(2,1)S(1)}, bf16[2,128,128]{2,1,0:T(8,128)(2,1)S(1)}, u32[]{:S(2)}, u32[]{:S(2)}) collective-permute-start(bf16[2,128,128]{2,1,0:T(8,128)(2,1)S(1)} %get-tuple-element.454), channel_id=1, source_target_pairs={{0,8},{8,16},{16,24},{24,32},{32,40},{40,48},{48,56},{56,64},{64,7... | collective-permute-start | bytes 196616 | tf_op jit(solution)/shard_map/while/body/eval_jaxpr/ppermute | solution.py:19
  29.9 4.6 collective-permute-start
  35.3 6.3 %collective-permute-start.1 = (bf16[2,128,128]{2,1,0:T(8,128)(2,1)S(1)}, bf16[2,128,128]{2,1,0:T(8,128)(2,1)S(1)}, u32[]{:S(2)}, u32[]{:S(2)}) collective-permute-start(bf16[2,128,128]{2,1,0:T(8,128)(2,1)S(1)} %get-tuple-element.454), channel_id=1, source_target_pairs={{0,8},{8,16},{16,24},{24,32},{32,40},{40,48},{48,56},{56,64},{64,7... | collective-permute-start | bytes 196616 | tf_op jit(solution)/shard_map/while/body/eval_jaxpr/ppermute | solution.py:19
  36.8 5.5 %collective-permute-start = (bf16[2,256,128]{2,1,0:T(8,128)(2,1)S(1)}, bf16[2,256,128]{2,1,0:T(8,128)(2,1)S(1)}, u32[]{:S(2)}, u32[]{:S(2)}) collective-permute-start(bf16[2,256,128]{2,1,0:T(8,128)(2,1)S(1)} %get-tuple-element.455), channel_id=1, source_target_pairs={{0,120},{8,0},{16,8},{24,16},{32,24},{40,32},{48,40},{56,48},{64,5... | collective-permute-start | bytes 393224 | tf_op jit(solution)/shard_map/while/body/eval_jaxpr/ppermute | solution.py:19
  43.2 6.3 %collective-permute-start.1 = (bf16[2,128,128]{2,1,0:T(8,128)(2,1)S(1)}, bf16[2,128,128]{2,1,0:T(8,128)(2,1)S(1)}, u32[]{:S(2)}, u32[]{:S(2)}) collective-permute-start(bf16[2,128,128]{2,1,0:T(8,128)(2,1)S(1)} %get-tuple-element.454), channel_id=1, source_target_pairs={{0,8},{8,16},{16,24},{24,32},{32,40},{40,48},{48,56},{56,64},{64,7... | collective-permute-start | bytes 196616 | tf_op jit(solution)/shard_map/while/body/eval_jaxpr/ppermute | solution.py:19
  43.8 6.3 %collective-permute-start = (bf16[2,256,128]{2,1,0:T(8,128)(2,1)S(1)}, bf16[2,256,128]{2,1,0:T(8,128)(2,1)S(1)}, u32[]{:S(2)}, u32[]{:S(2)}) collective-permute-start(bf16[2,256,128]{2,1,0:T(8,128)(2,1)S(1)} %get-tuple-element.455), channel_id=1, source_target_pairs={{0,120},{8,0},{16,8},{24,16},{32,24},{40,32},{48,40},{56,48},{64,5... | collective-permute-start | bytes 393224 | tf_op jit(solution)/shard_map/while/body/eval_jaxpr/ppermute | solution.py:19
  51.0 6.3 %collective-permute-start.1 = (bf16[2,128,128]{2,1,0:T(8,128)(2,1)S(1)}, bf16[2,128,128]{2,1,0:T(8,128)(2,1)S(1)}, u32[]{:S(2)}, u32[]{:S(2)}) collective-permute-start(bf16[2,128,128]{2,1,0:T(8,128)(2,1)S(1)} %get-tuple-element.454), channel_id=1, source_target_pairs={{0,8},{8,16},{16,24},{24,32},{32,40},{40,48},{48,56},{56,64},{64,7... | collective-permute-start | bytes 196616 | tf_op jit(solution)/shard_map/while/body/eval_jaxpr/ppermute | solution.py:19
  51.7 6.3 %collective-permute-start = (bf16[2,256,128]{2,1,0:T(8,128)(2,1)S(1)}, bf16[2,256,128]{2,1,0:T(8,128)(2,1)S(1)}, u32[]{:S(2)}, u32[]{:S(2)}) collective-permute-start(bf16[2,256,128]{2,1,0:T(8,128)(2,1)S(1)} %get-tuple-element.455), channel_id=1, source_target_pairs={{0,120},{8,0},{16,8},{24,16},{32,24},{40,32},{48,40},{56,48},{64,5... | collective-permute-start | bytes 393224 | tf_op jit(solution)/shard_map/while/body/eval_jaxpr/ppermute | solution.py:19
  58.9 6.3 %collective-permute-start.1 = (bf16[2,128,128]{2,1,0:T(8,128)(2,1)S(1)}, bf16[2,128,128]{2,1,0:T(8,128)(2,1)S(1)}, u32[]{:S(2)}, u32[]{:S(2)}) collective-permute-start(bf16[2,128,128]{2,1,0:T(8,128)(2,1)S(1)} %get-tuple-element.454), channel_id=1, source_target_pairs={{0,8},{8,16},{16,24},{24,32},{32,40},{40,48},{48,56},{56,64},{64,7... | collective-permute-start | bytes 196616 | tf_op jit(solution)/shard_map/while/body/eval_jaxpr/ppermute | solution.py:19
  59.5 6.3 %collective-permute-start = (bf16[2,256,128]{2,1,0:T(8,128)(2,1)S(1)}, bf16[2,256,128]{2,1,0:T(8,128)(2,1)S(1)}, u32[]{:S(2)}, u32[]{:S(2)}) collective-permute-start(bf16[2,256,128]{2,1,0:T(8,128)(2,1)S(1)} %get-tuple-element.455), channel_id=1, source_target_pairs={{0,120},{8,0},{16,8},{24,16},{32,24},{40,32},{48,40},{56,48},{64,5... | collective-permute-start | bytes 393224 | tf_op jit(solution)/shard_map/while/body/eval_jaxpr/ppermute | solution.py:19
  66.7 6.3 %collective-permute-start.1 = (bf16[2,128,128]{2,1,0:T(8,128)(2,1)S(1)}, bf16[2,128,128]{2,1,0:T(8,128)(2,1)S(1)}, u32[]{:S(2)}, u32[]{:S(2)}) collective-permute-start(bf16[2,128,128]{2,1,0:T(8,128)(2,1)S(1)} %get-tuple-element.454), channel_id=1, source_target_pairs={{0,8},{8,16},{16,24},{24,32},{32,40},{40,48},{48,56},{56,64},{64,7... | collective-permute-start | bytes 196616 | tf_op jit(solution)/shard_map/while/body/eval_jaxpr/ppermute | solution.py:19
  67.4 6.3 %collective-permute-start = (bf16[2,256,128]{2,1,0:T(8,128)(2,1)S(1)}, bf16[2,256,128]{2,1,0:T(8,128)(2,1)S(1)}, u32[]{:S(2)}, u32[]{:S(2)}) collective-permute-start(bf16[2,256,128]{2,1,0:T(8,128)(2,1)S(1)} %get-tuple-element.455), channel_id=1, source_target_pairs={{0,120},{8,0},{16,8},{24,16},{32,24},{40,32},{48,40},{56,48},{64,5... | collective-permute-start | bytes 393224 | tf_op jit(solution)/shard_map/while/body/eval_jaxpr/ppermute | solution.py:19
  74.6 6.3 %collective-permute-start.1 = (bf16[2,128,128]{2,1,0:T(8,128)(2,1)S(1)}, bf16[2,128,128]{2,1,0:T(8,128)(2,1)S(1)}, u32[]{:S(2)}, u32[]{:S(2)}) collective-permute-start(bf16[2,128,128]{2,1,0:T(8,128)(2,1)S(1)} %get-tuple-element.454), channel_id=1, source_target_pairs={{0,8},{8,16},{16,24},{24,32},{32,40},{40,48},{48,56},{56,64},{64,7... | collective-permute-start | bytes 196616 | tf_op jit(solution)/shard_map/while/body/eval_jaxpr/ppermute | solution.py:19
  75.2 6.3 %collective-permute-start = (bf16[2,256,128]{2,1,0:T(8,128)(2,1)S(1)}, bf16[2,256,128]{2,1,0:T(8,128)(2,1)S(1)}, u32[]{:S(2)}, u32[]{:S(2)}) collective-permute-start(bf16[2,256,128]{2,1,0:T(8,128)(2,1)S(1)} %get-tuple-element.455), channel_id=1, source_target_pairs={{0,120},{8,0},{16,8},{24,16},{32,24},{40,32},{48,40},{56,48},{64,5... | collective-permute-start | bytes 393224 | tf_op jit(solution)/shard_map/while/body/eval_jaxpr/ppermute | solution.py:19
  82.4 6.3 %collective-permute-start.1 = (bf16[2,128,128]{2,1,0:T(8,128)(2,1)S(1)}, bf16[2,128,128]{2,1,0:T(8,128)(2,1)S(1)}, u32[]{:S(2)}, u32[]{:S(2)}) collective-permute-start(bf16[2,128,128]{2,1,0:T(8,128)(2,1)S(1)} %get-tuple-element.454), channel_id=1, source_target_pairs={{0,8},{8,16},{16,24},{24,32},{32,40},{40,48},{48,56},{56,64},{64,7... | collective-permute-start | bytes 196616 | tf_op jit(solution)/shard_map/while/body/eval_jaxpr/ppermute | solution.py:19
  83.1 6.3 %collective-permute-start = (bf16[2,256,128]{2,1,0:T(8,128)(2,1)S(1)}, bf16[2,256,128]{2,1,0:T(8,128)(2,1)S(1)}, u32[]{:S(2)}, u32[]{:S(2)}) collective-permute-start(bf16[2,256,128]{2,1,0:T(8,128)(2,1)S(1)} %get-tuple-element.455), channel_id=1, source_target_pairs={{0,120},{8,0},{16,8},{24,16},{32,24},{40,32},{48,40},{56,48},{64,5... | collective-permute-start | bytes 393224 | tf_op jit(solution)/shard_map/while/body/eval_jaxpr/ppermute | solution.py:19
  90.3 6.3 %collective-permute-start.1 = (bf16[2,128,128]{2,1,0:T(8,128)(2,1)S(1)}, bf16[2,128,128]{2,1,0:T(8,128)(2,1)S(1)}, u32[]{:S(2)}, u32[]{:S(2)}) collective-permute-start(bf16[2,128,128]{2,1,0:T(8,128)(2,1)S(1)} %get-tuple-element.454), channel_id=1, source_target_pairs={{0,8},{8,16},{16,24},{24,32},{32,40},{40,48},{48,56},{56,64},{64,7... | collective-permute-start | bytes 196616 | tf_op jit(solution)/shard_map/while/body/eval_jaxpr/ppermute | solution.py:19
  90.9 6.3 %collective-permute-start = (bf16[2,256,128]{2,1,0:T(8,128)(2,1)S(1)}, bf16[2,256,128]{2,1,0:T(8,128)(2,1)S(1)}, u32[]{:S(2)}, u32[]{:S(2)}) collective-permute-start(bf16[2,256,128]{2,1,0:T(8,128)(2,1)S(1)} %get-tuple-element.455), channel_id=1, source_target_pairs={{0,120},{8,0},{16,8},{24,16},{32,24},{40,32},{48,40},{56,48},{64,5... | collective-permute-start | bytes 393224 | tf_op jit(solution)/shard_map/while/body/eval_jaxpr/ppermute | solution.py:19
  98.1 6.4 %collective-permute-start.1 = (bf16[2,128,128]{2,1,0:T(8,128)(2,1)S(1)}, bf16[2,128,128]{2,1,0:T(8,128)(2,1)S(1)}, u32[]{:S(2)}, u32[]{:S(2)}) collective-permute-start(bf16[2,128,128]{2,1,0:T(8,128)(2,1)S(1)} %get-tuple-element.454), channel_id=1, source_target_pairs={{0,8},{8,16},{16,24},{24,32},{32,40},{40,48},{48,56},{56,64},{64,7... | collective-permute-start | bytes 196616 | tf_op jit(solution)/shard_map/while/body/eval_jaxpr/ppermute | solution.py:19
  98.8 6.4 %collective-permute-start = (bf16[2,256,128]{2,1,0:T(8,128)(2,1)S(1)}, bf16[2,256,128]{2,1,0:T(8,128)(2,1)S(1)}, u32[]{:S(2)}, u32[]{:S(2)}) collective-permute-start(bf16[2,256,128]{2,1,0:T(8,128)(2,1)S(1)} %get-tuple-element.455), channel_id=1, source_target_pairs={{0,120},{8,0},{16,8},{24,16},{32,24},{40,32},{48,40},{56,48},{64,5... | collective-permute-start | bytes 393224 | tf_op jit(solution)/shard_map/while/body/eval_jaxpr/ppermute | solution.py:19
  106.0 6.3 %collective-permute-start.1 = (bf16[2,128,128]{2,1,0:T(8,128)(2,1)S(1)}, bf16[2,128,128]{2,1,0:T(8,128)(2,1)S(1)}, u32[]{:S(2)}, u32[]{:S(2)}) collective-permute-start(bf16[2,128,128]{2,1,0:T(8,128)(2,1)S(1)} %get-tuple-element.454), channel_id=1, source_target_pairs={{0,8},{8,16},{16,24},{24,32},{32,40},{40,48},{48,56},{56,64},{64,7... | collective-permute-start | bytes 196616 | tf_op jit(solution)/shard_map/while/body/eval_jaxpr/ppermute | solution.py:19
  106.7 6.3 %collective-permute-start = (bf16[2,256,128]{2,1,0:T(8,128)(2,1)S(1)}, bf16[2,256,128]{2,1,0:T(8,128)(2,1)S(1)}, u32[]{:S(2)}, u32[]{:S(2)}) collective-permute-start(bf16[2,256,128]{2,1,0:T(8,128)(2,1)S(1)} %get-tuple-element.455), channel_id=1, source_target_pairs={{0,120},{8,0},{16,8},{24,16},{32,24},{40,32},{48,40},{56,48},{64,5... | collective-permute-start | bytes 393224 | tf_op jit(solution)/shard_map/while/body/eval_jaxpr/ppermute | solution.py:19
  113.9 6.3 %collective-permute-start.1 = (bf16[2,128,128]{2,1,0:T(8,128)(2,1)S(1)}, bf16[2,128,128]{2,1,0:T(8,128)(2,1)S(1)}, u32[]{:S(2)}, u32[]{:S(2)}) collective-permute-start(bf16[2,128,128]{2,1,0:T(8,128)(2,1)S(1)} %get-tuple-element.454), channel_id=1, source_target_pairs={{0,8},{8,16},{16,24},{24,32},{32,40},{40,48},{48,56},{56,64},{64,7... | collective-permute-start | bytes 196616 | tf_op jit(solution)/shard_map/while/body/eval_jaxpr/ppermute | solution.py:19
  115.6 5.3 %collective-permute-start = (bf16[2,256,128]{2,1,0:T(8,128)(2,1)S(1)}, bf16[2,256,128]{2,1,0:T(8,128)(2,1)S(1)}, u32[]{:S(2)}, u32[]{:S(2)}) collective-permute-start(bf16[2,256,128]{2,1,0:T(8,128)(2,1)S(1)} %get-tuple-element.455), channel_id=1, source_target_pairs={{0,120},{8,0},{16,8},{24,16},{32,24},{40,32},{48,40},{56,48},{64,5... | collective-permute-start | bytes 393224 | tf_op jit(solution)/shard_map/while/body/eval_jaxpr/ppermute | solution.py:19
  121.8 6.3 %collective-permute-start.1 = (bf16[2,128,128]{2,1,0:T(8,128)(2,1)S(1)}, bf16[2,128,128]{2,1,0:T(8,128)(2,1)S(1)}, u32[]{:S(2)}, u32[]{:S(2)}) collective-permute-start(bf16[2,128,128]{2,1,0:T(8,128)(2,1)S(1)} %get-tuple-element.454), channel_id=1, source_target_pairs={{0,8},{8,16},{16,24},{24,32},{32,40},{40,48},{48,56},{56,64},{64,7... | collective-permute-start | bytes 196616 | tf_op jit(solution)/shard_map/while/body/eval_jaxpr/ppermute | solution.py:19
  134.2 31.9 %all-to-all-start = ((f32[8,16,4096]{2,1,0:T(8,128)}), f32[8,16,4096]{2,1,0:T(8,128)S(1)}, u32[]{:S(2)}, u32[]{:S(2)}) async-start(f32[8,16,4096]{2,1,0:T(8,128)} %fusion.34), calls=%async_computation | async-start | bytes 4194304 | tf_op jit(solution)/shard_map/all_to_all | solution.py:29
  140.3 170.7 %all-gather.2.cloned.1.call-start = ((), (), s32[]{:S(2)}) async-start(), calls=%async_computation.4 | async-start | bytes 17825792 | tf_op jit(solution)/shard_map/all_gather | solution.py:48
  189.1 247.6 %reduce-scatter.2.cloned.1.call-start = ((), (), s32[]{:S(2)}) async-start(), calls=%async_computation.5 | async-start | bytes 8912896 | tf_op jit(solution)/shard_map/reduce_scatter | solution.py:202
  436.7 15.1 %all-to-all-start.2 = ((bf16[8,8,4096]{2,1,0:T(8,128)(2,1)}), bf16[8,8,4096]{2,1,0:T(8,128)(2,1)S(1)}, u32[]{:S(2)}, u32[]{:S(2)}) async-start(bf16[8,8,4096]{2,1,0:T(8,128)(2,1)} %bitcast.141), calls=%async_computation.3 | async-start | bytes 1048576 | tf_op jit(solution)/shard_map/all_to_all | solution.py:208
  (11 other events, 313.6 us)
Sparse Core Ops, SparseCore 0:
  189.2 121.8 all-gather.1
  335.5 101.1 reduce-scatter.1
where the time goes:
time: 460 us; the launch traced here: 459 us
  waiting for transfers between devices  284 us (62%)
  starting transfers between devices  77.4 us (17%)
  matrix products  50.5 us (11%)
  blocking collectives  20.4 us (4%)
  between operations  14.3 us (3%)
  other arithmetic  6.83 us (1%)
  local copies, waits for them, and re-layouts  5.02 us (1%)
    all_gather x1, waiting for transfers between devices, in_one_piece(): lax.all_gather(both, axis, axis=dim, tiled=True)  122 us
    reduce_scatter x1, waiting for transfers between devices, on_device(): lax.psum_scatter(jnp.dot(hidden_all, down_mat, preferred_element_type=jnp...  101 us
    ppermute x30, starting transfers between devices, from_behind(): lax.ppermute(shard, axis, [(i, (i + by) % devices) for i in range(devices)])  66.3 us
    ppermute x30, waiting for transfers between devices, from_behind(): lax.ppermute(shard, axis, [(i, (i + by) % devices) for i in range(devices)])  35.4 us
    all_to_all x1, waiting for transfers between devices, summed_on_arrival(): lax.all_to_all(blocks, axis, split_axis=0, concat_axis=0, tiled=True)  25.2 us
    all_to_all x1, blocking collectives, sent_together(): lax.all_to_all(both, axis, split_axis=split_dim, concat_axis=concat_dim,...  20.4 us
    dot_general x1, matrix products, on_device(): gate_val = jnp.dot(rows_all, gate_mat, preferred_element_type=jnp.float32)  10.5 us
    dot_general x1, matrix products, on_device(): lax.dot_general(hidden_all, grads_all, (((0,), (0,)), ((), ())), preferre...  10.2 us
  transfers between devices with their start and end apart: 34, of which 33 were waited for; matrix products, arithmetic and copies ran while one was open for 3% of the time, Pallas kernels for 0%

commit v1 on v0

v1 whole, which is shorter than its diff:
```python
import functools
import math

import jax
import jax.numpy as jnp
from jax import lax
from jax.experimental import pallas as pl
from jax.experimental.pallas import tpu as pltpu
from jax.sharding import PartitionSpec as P

QUERY_HEADS = 32
KEY_VALUE_HEADS = 8
HEAD_SIZE = 128
WINDOW = 4096
MESH = pl.DeviceIdType.MESH
N_CTX = 16
N_EXP = 8
D = 4096
GROUPS = QUERY_HEADS // KEY_VALUE_HEADS
TOKENS = 128
PRIOR = 256
KEYS = PRIOR + TOKENS
ROWS = 16
CAP = 8
SLOTS = N_EXP * CAP
SCALE = 1.0 / math.sqrt(HEAD_SIZE)
BF16 = jnp.bfloat16
F32 = jnp.float32

epsilon = 1e-05

COPIES = {
    0: (0, 0, "P", None),
    1: (0, 0, "Z", None),
    2: (0, 0, "R", None),
    3: (0, 0, "L", None),
    4: (0, 1, "P", None),
    5: (0, 1, "R", None),
    6: (0, 1, "L", None),
    7: (-1, 0, "P", None),
    8: (-1, 0, "R", 0),
    9: (1, 0, "P", None),
    10: (1, 0, "L", 1),
    11: (2, 0, "P", None),
    12: (-1, 1, "P", None),
    13: (-1, 1, "R", 0),
    14: (1, 1, "P", None),
    15: (1, 1, "L", 1),
    16: (2, 1, "P", None),
}


class Place:
    def __init__(self):
        self.c = lax.axis_index("ctx")
        self.e = lax.axis_index("exp")
        self.x = self.c // 4
        self.z = (self.c // 2) % 2
        self.k = self.c % 2

    def block(self, dx, dz, dk=0):
        return ((self.x + dx + 4) % 4) * 4 + ((self.z + dz) % 2) * 2 + (self.k + dk) % 2

    def peer(self, to):
        at = {"P": (0, 0, 1), "Z": (0, 1, 0), "R": (1, 0, 0), "L": (-1, 0, 0)}[to]
        return (self.block(*at), self.e)

    def expert(self, by):
        return (self.e + by) % N_EXP


class Gather:
    def __init__(self, place, part_of, send, recv):
        self.p, self.part_of, self.send, self.recv = place, part_of, send, recv

    def copy(self, i, arriving):
        dx, dz, to, half = COPIES[i]
        dk = 0
        if arriving:
            if to == "P":
                dk = 1
            elif to == "Z":
                dz = 1 - dz
            elif to == "R":
                dx = dx - 1
            else:
                dx = dx + 1
        ref = self.part_of(self.p.block(dx, dz, dk), half)
        return pltpu.make_async_remote_copy(
            src_ref=ref,
            dst_ref=ref,
            send_sem=self.send.at[i],
            recv_sem=self.recv.at[i],
            device_id=self.p.peer(to),
            device_id_type=MESH,
        )

    def start(self, *ids):
        for i in ids:
            self.copy(i, False).start()

    def wait(self, *ids):
        for i in ids:
            self.copy(i, True).wait_recv()

    def drain(self):
        for i in COPIES:
            self.copy(i, False).wait_send()


def greet(place):
    barrier = pltpu.get_barrier_semaphore()
    peers = [place.peer(to) for to in ("P", "Z", "R", "L")]
    peers += [(place.c, place.expert(j)) for j in range(1, N_EXP)]
    for peer in peers:
        pl.semaphore_signal(barrier, inc=1, device_id=peer, device_id_type=MESH)
    pl.semaphore_wait(barrier, len(peers))


def attention_kernel(
    q_ref, kv_hbm, cache_hbm, w_hbm, cot_ref,
    out_ref, cot_out,
    kv, w, cot, attn, peak, total, mixed, parts, arrived,
    local, kv_send, kv_recv, cot_send, cot_recv, to_send, to_recv, sum_send, sum_recv, put,
):
    place = Place()
    c, e = place.c, place.e
    mine = pl.ds(pl.multiple_of(e * CAP, CAP), CAP)
    loads = [
        pltpu.make_async_copy(cache_hbm, kv.at[c, :, pl.ds(0, PRIOR)], local.at[0]),
        pltpu.make_async_copy(kv_hbm, kv.at[c, :, pl.ds(PRIOR, TOKENS)], local.at[1]),
        pltpu.make_async_copy(cot_ref.at[e], cot.at[c, mine], local.at[2]),
        pltpu.make_async_copy(w_hbm, w, local.at[3]),
    ]
    for load in loads:
        load.start()
    greet(place)

    def kv_part(b, half):
        return kv.at[b] if half is None else kv.at[b, half]

    def cot_part(b, half):
        return cot.at[b] if half is None else cot.at[b, pl.ds(half * 32, 32)]

    keys = Gather(place, kv_part, kv_send, kv_recv)
    cots = Gather(place, cot_part, cot_send, cot_recv)

    def to_expert(j, arriving):
        if arriving:
            at = pl.ds(pl.multiple_of(place.expert(N_EXP - j) * CAP, CAP), CAP)
        else:
            at = mine
        return pltpu.make_async_remote_copy(
            src_ref=cot_ref.at[place.expert(j)],
            dst_ref=cot.at[c, at],
            send_sem=to_send.at[j],
            recv_sem=to_recv.at[j],
            device_id=(c, place.expert(j)),
            device_id_type=MESH,
        )

    loads[0].wait()
    loads[1].wait()
    keys.start(1, 2, 3, 0)
    for j in range(1, N_EXP):
        to_expert(j, False).start()

    peak[...] = jnp.full(peak.shape, -1e30, F32)
    total[...] = jnp.zeros(total.shape, F32)
    mixed[...] = jnp.zeros(mixed.shape, F32)
    token = c * TOKENS + lax.broadcasted_iota(jnp.int32, (TOKENS, 1), 0)

    def attend(dx):
        first = place.block(dx, 0) // 4 * 4
        lane = lax.broadcasted_iota(jnp.int32, (1, 4 * KEYS), 1)
        number = (
            (lane >= KEYS).astype(jnp.int32)
            + (lane >= 2 * KEYS).astype(jnp.int32)
            + (lane >= 3 * KEYS).astype(jnp.int32)
        )
        inside = lane - number * KEYS
        owner = first + number
        old = inside < PRIOR
        below = jnp.where(old, owner * PRIOR + inside, 1 << 30)
        above = jnp.where(old, -1, owner * TOKENS + inside - PRIOR)
        visible = (token < below) & (token >= above)
        offset = jnp.where(visible, 0.0, -1e30)

        @pl.loop(0, GROUPS)
        def _(h):
            key_rows = kv[pl.ds(first, 4), 0].reshape(4 * KEYS, HEAD_SIZE)
            value_rows = kv[pl.ds(first, 4), 1].reshape(4 * KEYS, HEAD_SIZE)
            scores = lax.dot_general(
                q_ref[h], key_rows, (((1,), (1,)), ((), ())), preferred_element_type=F32
            )
            scores = scores * SCALE + offset
            old_peak = peak[h][:, :1]
            new_peak = jnp.maximum(old_peak, jnp.max(scores, axis=-1, keepdims=True))
            weights = jnp.exp(scores - new_peak)
            rescale = jnp.exp(old_peak - new_peak)
            sums = total[h][:, :1] * rescale + jnp.sum(weights, axis=-1, keepdims=True)
            peak[h] = jnp.broadcast_to(new_peak, (TOKENS, HEAD_SIZE))
            total[h] = jnp.broadcast_to(sums, (TOKENS, HEAD_SIZE))
            mixed[h] = mixed[h] * rescale + jnp.dot(
                weights.astype(BF16), value_rows, preferred_element_type=F32
            )

    keys.wait(0, 2)
    keys.start(8, 7)
    keys.wait(3)
    keys.start(10, 9)
    keys.wait(1)
    keys.start(5, 6, 4)
    loads[2].wait()
    for j in range(1, N_EXP):
        to_expert(j, True).wait_recv()
    cots.start(1, 2, 3, 0)
    keys.wait(4)
    attend(0)
    keys.wait(5)
    keys.start(13, 12)
    keys.wait(6)
    keys.start(15, 14)
    keys.wait(8, 10)
    keys.start(11)
    keys.wait(7, 12)
    attend(-1)
    keys.wait(9, 14)
    keys.wait(13, 15)
    keys.start(16)
    attend(1)
    cots.wait(0, 2)
    cots.start(8, 7)
    cots.wait(3)
    cots.start(10, 9)
    keys.wait(11, 16)
    attend(2)

    for h in range(GROUPS):
        attn[:, h * HEAD_SIZE : (h + 1) * HEAD_SIZE] = (mixed[h] / total[h]).astype(BF16)
    loads[3].wait()

    @pl.loop(0, 8)
    def _(n):
        at = pl.ds(pl.multiple_of(n * 512, 512), 512)
        tile = jnp.dot(attn[...], w[:, at], preferred_element_type=F32)
        parts[:, :, at] = tile.astype(BF16).reshape(N_EXP, ROWS, 512)

    def to_owner(j, arriving):
        return pltpu.make_async_remote_copy(
            src_ref=parts.at[place.expert(j)],
            dst_ref=arrived.at[place.expert(N_EXP - j) if arriving else e],
            send_sem=sum_send.at[j],
            recv_sem=sum_recv.at[j],
            device_id=(c, place.expert(j)),
            device_id_type=MESH,
        )

    for j in range(1, N_EXP):
        to_owner(j, False).start()
    cots.wait(1)
    cots.start(5, 6, 4)
    cots.wait(8, 10)
    cots.start(11)
    for j in range(1, N_EXP):
        to_owner(j, True).wait_recv()

    @pl.loop(0, 8)
    def _(n):
        at = pl.ds(pl.multiple_of(n * 512, 512), 512)
        acc = parts[e, :, at].astype(F32)
        for j in range(1, N_EXP):
            acc = acc + arrived[place.expert(j), :, at].astype(F32)
        out_ref[:, at] = acc

    cots.wait(5)
    cots.start(13, 12)
    cots.wait(6)
    cots.start(15, 14)
    cots.wait(13, 15)
    cots.start(16)
    cots.wait(4, 7, 9, 11, 12, 14, 16)
    stores = [pltpu.make_async_copy(cot, cot_out, put)]
    for store in stores:
        store.start()
    for store in stores:
        store.wait()
    keys.drain()
    cots.drain()
    for j in range(1, N_EXP):
        to_expert(j, False).wait_send()
        to_owner(j, False).wait_send()


def attend_and_project(query, keys_values, cache, out_proj, cot_slots):
    queries = jnp.transpose(query.reshape(TOKENS, GROUPS, HEAD_SIZE), (1, 0, 2))
    hbm = pl.BlockSpec(memory_space=pl.ANY)
    vmem = pl.BlockSpec(memory_space=pltpu.VMEM)
    dma = pltpu.SemaphoreType.DMA
    n = len(COPIES)
    return pl.pallas_call(
        attention_kernel,
        out_shape=(
            jax.ShapeDtypeStruct((ROWS, D), F32),
            jax.ShapeDtypeStruct((N_CTX, SLOTS, D), BF16),
        ),
        in_specs=[vmem, hbm, hbm, hbm, vmem],
        out_specs=(vmem, hbm),
        scratch_shapes=[
            pltpu.VMEM((N_CTX, 2, KEYS, HEAD_SIZE), BF16),
            pltpu.VMEM((GROUPS * HEAD_SIZE, D), BF16),
            pltpu.VMEM((N_CTX, SLOTS, D), BF16),
            pltpu.VMEM((TOKENS, GROUPS * HEAD_SIZE), BF16),
            pltpu.VMEM((GROUPS, TOKENS, HEAD_SIZE), F32),
            pltpu.VMEM((GROUPS, TOKENS, HEAD_SIZE), F32),
            pltpu.VMEM((GROUPS, TOKENS, HEAD_SIZE), F32),
            pltpu.VMEM((N_EXP, ROWS, D), BF16),
            pltpu.VMEM((N_EXP, ROWS, D), BF16),
            dma((4,)),
            dma((n,)),
            dma((n,)),
            dma((n,)),
            dma((n,)),
            dma((N_EXP,)),
            dma((N_EXP,)),
            dma((N_EXP,)),
            dma((N_EXP,)),
            dma,
        ],
        compiler_params=pltpu.CompilerParams(
            collective_id=0, has_side_effects=True, vmem_limit_bytes=48 * 1024 * 1024
        ),
        name="attention_kernel",
    )(queries, keys_values, cache, out_proj, cot_slots)


def experts_part(outgoing, weighted_rows, cot_all, gate_mat, up_mat, down_mat, hidden_one):
    gate_col = jnp.sum(weighted_rows, axis=-1, keepdims=True)
    high = gate_col.astype(BF16)
    low = (gate_col - high.astype(F32)).astype(BF16)
    extra = jnp.concatenate([high, low, jnp.zeros((SLOTS, 126), BF16)], axis=1)
    both = jnp.concatenate([outgoing, extra], axis=1).reshape(N_EXP, CAP, D + 128)
    arrived = lax.all_to_all(both, "exp", split_axis=0, concat_axis=0, tiled=True)
    rows_all = lax.all_gather(arrived.reshape(SLOTS, D + 128), "ctx", axis=0, tiled=True)
    gate_all = rows_all[:, D].astype(F32) + rows_all[:, D + 1].astype(F32)
    rows_all = rows_all[:, :D]
    gate_val = jnp.dot(rows_all, gate_mat, preferred_element_type=F32)
    up_val = jnp.dot(rows_all, up_mat, preferred_element_type=F32)
    hidden_all = (jax.nn.silu(gate_val) * up_val).astype(BF16)
    expert_out = lax.psum_scatter(
        jnp.dot(hidden_all, down_mat, preferred_element_type=F32).astype(BF16),
        "ctx",
        scatter_dimension=0,
        tiled=True,
    )
    returned = lax.all_to_all(
        expert_out.reshape(N_EXP, CAP, D), "exp", split_axis=0, concat_axis=0, tiled=True
    )
    combined = jnp.dot(weighted_rows.T, returned.reshape(SLOTS, D).astype(F32))
    layer_out = (hidden_one + combined).astype(BF16)
    gated = (gate_all[:, None] * hidden_all.astype(F32)).astype(BF16)
    gradient = lax.dot_general(
        gated, cot_all.reshape(N_CTX * SLOTS, D), (((0,), (0,)), ((), ())), preferred_element_type=F32
    )
    return (layer_out, gradient[None])


def on_device(
    query,
    keys_values,
    cache,
    residual,
    out_proj,
    norm_gain,
    router,
    expert_ids,
    w_gate,
    w_up,
    w_down,
    cotangent,
):
    experts = router.shape[1]
    onehot = (expert_ids[:, :, None] == jnp.arange(experts, dtype=jnp.int32)[None, None, :]).astype(F32)
    assigned = ROWS * 2
    flat_hot = onehot.reshape(assigned, experts)
    earlier = (jnp.arange(assigned)[:, None] > jnp.arange(assigned)[None, :]).astype(F32)
    before = jnp.dot(earlier, flat_hot)
    slot = jnp.sum(before * flat_hot, axis=-1).astype(jnp.int32)
    target = expert_ids.reshape(assigned) * CAP + slot
    dispatch = (jnp.arange(SLOTS, dtype=jnp.int32)[:, None] == target[None, :]).astype(F32)
    dispatch = dispatch.reshape(SLOTS, ROWS, 2)
    pick_rows = jnp.sum(dispatch, axis=-1)
    picks = pick_rows.astype(BF16)
    cot_slots = jnp.dot(picks, cotangent, preferred_element_type=F32).astype(BF16)
    cot_slots = cot_slots.reshape(experts, CAP, D)

    projected, cot_all = attend_and_project(query, keys_values, cache, out_proj, cot_slots)

    hidden_one = residual.astype(F32) + projected
    mean_square = jnp.mean(hidden_one * hidden_one, axis=-1, keepdims=True)
    normed = (hidden_one * lax.rsqrt(mean_square + epsilon) * norm_gain).astype(BF16)
    logits = jnp.dot(normed, router, preferred_element_type=F32)
    chosen = jnp.sum(onehot * logits[:, None, :], axis=-1)
    first = 1.0 / (1.0 + jnp.exp(chosen[:, 1] - chosen[:, 0]))
    gates = jnp.stack([first, 1.0 - first], axis=1)
    weighted_rows = jnp.sum(dispatch * gates[None, :, :], axis=-1)
    outgoing = jnp.dot(picks, normed, preferred_element_type=F32).astype(BF16)
    return experts_part(
        outgoing, weighted_rows, cot_all, w_gate[0], w_up[0], w_down[0], hidden_one
    )


def solution(mesh):
    placed = (
        P("ctx", "exp"),
        P(None, "ctx", "exp"),
        P(None, "ctx", "exp"),
        P(("ctx", "exp"), None),
        P("exp", None),
        P(),
        P(),
        P(("ctx", "exp"), None),
        P("exp", None, "ctx"),
        P("exp", None, "ctx"),
        P("exp", "ctx", None),
        P(("ctx", "exp"), None),
    )
    return jax.shard_map(
        on_device,
        mesh=mesh,
        in_specs=placed,
        out_specs=(P(("ctx", "exp"), None), P("exp", "ctx", None)),
        check_vma=False,
    )
```

time: 460 us -> 317 us (0.69)
  waiting for transfers between devices: 284 us -> 172 us
  starting transfers between devices: 77.4 us -> 4.95 us
  Pallas kernels: 0 us -> 64.9 us
  matrix products: 50.5 us -> 31.8 us
    ppermute x30 -> x0, starting transfers between devices: 66.3 us -> none  [from_behind(): lax.ppermute(shard, axis, [(i, (i + by) % devices) for i in range(devices)])]
    pallas_call x0 -> x1, Pallas kernels: none -> 64.9 us  [attend_and_project(): pl.pallas_call(attention_kernel, out_shape=(jax.ShapeDtypeStruct((ROWS, D...]
    all_gather x1, waiting for transfers between devices: 122 us -> 72.3 us  [experts_part(): lax.all_gather(arrived.reshape(SLOTS, D + 128), 'ctx', axis=0, tiled=True)]
    ppermute x30 -> x0, waiting for transfers between devices: 35.4 us -> none  [from_behind(): lax.ppermute(shard, axis, [(i, (i + by) % devices) for i in range(devices)])]
    all_to_all x2 -> x1, waiting for transfers between devices: 25.2 us -> 0.01 us  [experts_part(): lax.all_to_all(expert_out.reshape(N_EXP, CAP, D), 'exp', split_axis=0, co...]
    dot_general x41 -> x8, matrix products: 50.4 us -> 31.7 us  [the longest x1 10.4 us: experts_part(): lax.dot_general(gated, cot_all.reshape(N_CTX * SLOTS, D), (((0,), (0,)),...]
    all_to_all x2 -> x1, starting transfers between devices: 11 us -> 4.87 us  [experts_part(): lax.all_to_all(expert_out.reshape(N_EXP, CAP, D), 'exp', split_axis=0, co...]
  transfers between devices with their start and end apart: 34 -> 3, of which waited for: 33 -> 2; matrix products, arithmetic and copies ran while one was open for 3% -> 4% of each run, Pallas kernels for 0% -> 0%
where the time goes in v1:
time: 317 us; the launch traced here: 316 us
  waiting for transfers between devices  172 us (54%)
  Pallas kernels  64.9 us (20%)
  matrix products  31.8 us (10%)
  blocking collectives  18.3 us (6%)
  between operations  14.2 us (4%)
  local copies, waits for them, and re-layouts  6.84 us (2%)
  starting transfers between devices  4.95 us (2%)
    reduce_scatter x1, waiting for transfers between devices, experts_part(): lax.psum_scatter(jnp.dot(hidden_all, down_mat, preferred_element_type=F32...  99.9 us
    all_gather x1, waiting for transfers between devices, experts_part(): lax.all_gather(arrived.reshape(SLOTS, D + 128), 'ctx', axis=0, tiled=True)  72.3 us
    pallas_call x1, Pallas kernels, attend_and_project(): pl.pallas_call(attention_kernel, out_shape=(jax.ShapeDtypeStruct((ROWS, D...  64.9 us
    all_to_all x1, blocking collectives, experts_part(): lax.all_to_all(both, 'exp', split_axis=0, concat_axis=0, tiled=True)  18.3 us
    dot_general x1, matrix products, experts_part(): lax.dot_general(gated, cot_all.reshape(N_CTX * SLOTS, D), (((0,), (0,)),...  10.4 us
    dot_general x1, matrix products, experts_part(): gate_val = jnp.dot(rows_all, gate_mat, preferred_element_type=F32)  8.27 us
    dot_general x1, matrix products, experts_part(): jnp.dot(hidden_all, down_mat, preferred_element_type=F32).astype(BF16)  6.73 us
  transfers between devices with their start and end apart: 3, of which 2 were waited for; matrix products, arithmetic and copies ran while one was open for 4% of the time, Pallas kernels for 0%

profile of v1, /device:TPU:26, one launch (start us, length us, event | category | flops | bytes accessed | tf_op | source)
XLA Modules:
  0.0 315.9 jit_solution(14422658741084795957)
XLA Ops:
  7.3 0.8 copy.60
  8.1 0.1 eq.38
  8.2 0.1 fusion.14
  8.4 0.1 convert_element_type.99
  8.4 0.1 copy.61
  8.5 0.7 multiply_add_fusion
  9.3 1.0 copy.58
  10.3 0.1 copy.59
  10.5 0.3 fusion.4.cot_ref
  10.8 2.2 copy-done.1
  13.0 0.9 copy-done.2
  13.9 0.8 copy-done.3
  14.7 64.9 %attention_kernel.1 = (f32[16,4096]{1,0:T(8,128)S(1)}, bf16[16,64,4096]{2,1,0:T(8,128)(2,1)}) custom-call(bf16[4,128,128]{2,1,0:T(8,128)(2,1)S(1)} %bitcast.34, bf16[2,128,128]{2,1,0:T(8,128)(2,1)S(1)} %copy-done.3, bf16[2,256,128]{2,1,0:T(8,128)(2,1)S(1)} %copy-done.2, bf16[512,4096]{1,0:T(8,128)(2,1)S(1)} %copy-done.1, bf16[8,8,4096]{2,1,0:T(8,128)(2,1)S(1)} %fusion.4.cot_ref), custom_call_target="tpu_custom_call" | custom-call | tf_op jit(solution)/shard_map/attention_kernel/pallas_call | solution.py:301
  79.7 0.2 multiply_reduce_fusion
  79.8 0.1 multiply_convert_fusion.3
  79.9 0.3 fusion.5
  80.3 0.1 fusion.20
  80.5 0.1 select_reduce_fusion
  80.6 0.1 reduce_sum.62
  80.7 0.1 copy.62
  80.8 0.1 copy.63
  80.9 0.3 concatenate.7
  81.2 18.3 %all_to_all.10 = bf16[8,8,4224]{2,1,0:T(8,128)(2,1)} all-to-all(bf16[8,8,4224]{2,1,0:T(8,128)(2,1)S(1)} %concatenate.7), channel_id=1, replica_groups=mesh['ctx'=16,'exp'=8] {'exp'}, dimensions={0} | all-to-all | bytes 1081344 | tf_op jit(solution)/shard_map/all_to_all | solution.py:343
  99.5 72.3 %all-gather.2.cloned.1.call-done = bf16[1024,4224]{1,0:T(8,128)(2,1)} async-done(((bf16[64,4224]{1,0:T(8,128)(2,1)}), bf16[1024,4224]{1,0:T(8,128)(2,1)}) %all-gather.2.cloned.1.call-update) | async-done | bytes 8650768 | tf_op jit(solution)/shard_map/all_gather | solution.py:344
  171.9 8.3 %fusion.2 = f32[1024,512]{1,0:T(8,128)S(1)} fusion(bf16[1024,4224]{1,0:T(8,128)(2,1)} %all-gather.2.cloned.1.call-done, bf16[1,4096,512]{2,1,0:T(8,128)(2,1)} %param.20), kind=kOutput, calls=%fused_computation.3 | convolution fusion | flops 4294967296 | bytes 14680064 | tf_op jit(solution)/shard_map/dot_general | solution.py:347
  180.2 4.7 %multiply_convert_fusion.1 = bf16[1024,512]{1,0:T(8,128)(2,1)S(1)} fusion(f32[1024,512]{1,0:T(8,128)S(1)} %fusion.2, bf16[1,4096,512]{2,1,0:T(8,128)(2,1)S(1)} %copy-done.9, bf16[1024,4224]{1,0:T(8,128)(2,1)S(1)} %copy-done.6), kind=kOutput, calls=%fused_computation.16 | convolution fusion | flops 4298113024 | bytes 15728640 | tf_op jit(solution)/shard_map/dot_general | solution.py:348
  184.9 6.7 %convolution_convert_fusion = bf16[1024,4096]{1,0:T(8,128)(2,1)} fusion(bf16[1024,512]{1,0:T(8,128)(2,1)S(1)} %multiply_convert_fusion.1, bf16[1,512,4096]{2,1,0:T(8,128)(2,1)S(1)} %copy-done.10), kind=kOutput, calls=%fused_computation | convolution fusion | flops 4299161600 | bytes 13631488 | tf_op jit(solution)/shard_map/dot_general | solution.py:351
  191.7 1.3 add_reduce_fusion
  193.0 99.9 %reduce-scatter.2.cloned.1.call-done = bf16[64,4096]{1,0:T(8,128)(2,1)} async-done(((bf16[1024,4096]{1,0:T(8,128)(2,1)}), bf16[64,4096]{1,0:T(8,128)(2,1)}) %reduce-scatter.2.cloned.1.call-update) | async-done | bytes 524304 | tf_op jit(solution)/shard_map/reduce_scatter | solution.py:350
  292.9 4.9 %all-to-all-start.1 = ((bf16[8,8,4096]{2,1,0:T(8,128)(2,1)}), bf16[8,8,4096]{2,1,0:T(8,128)(2,1)S(1)}, u32[]{:S(2)}, u32[]{:S(2)}) async-start(bf16[8,8,4096]{2,1,0:T(8,128)(2,1)} %bitcast.37), calls=%async_computation.2 | async-start | bytes 1048576 | tf_op jit(solution)/shard_map/all_to_all | solution.py:356
  297.8 10.4 %convolution_bitcast_fusion = f32[1,512,4096]{2,1,0:T(8,128)} fusion(bf16[1024,4096]{1,0:T(8,128)(2,1)} %bitcast.35, bf16[1024,512]{1,0:T(8,128)(2,1)S(1)} %multiply_convert_fusion.1, f32[1024]{0:T(1024)S(1)} %add_reduce_fusion), kind=kOutput, calls=%fused_computation.5 | convolution fusion | flops 4296540160 | bytes 17829888 | tf_op jit(solution)/shard_map/dot_general | solution.py:362
  308.2 0.9 fusion.6
  (32 shorter events, 0.3 us)
Async XLA Ops:
  7.2 3.3 %copy-start = (bf16[16,4096]{1,0:T(8,128)(2,1)S(1)}, bf16[16,4096]{1,0:T(8,128)(2,1)}, u32[]{:S(2)}) copy-start(bf16[16,4096]{1,0:T(8,128)(2,1)} %param.23) | copy-start | bytes 393220
  7.2 73.2 %copy-start.8 = (s32[16,2]{0,1:T(2,128)S(1)}, s32[16,2]{0,1:T(2,128)}, u32[]{:S(2)}) copy-start(s32[16,2]{0,1:T(2,128)} %param.19) | copy-start | bytes 388
  7.2 72.5 %copy-start.4 = (bf16[16,4096]{1,0:T(8,128)(2,1)S(1)}, bf16[16,4096]{1,0:T(8,128)(2,1)}, u32[]{:S(2)}) copy-start(bf16[16,4096]{1,0:T(8,128)(2,1)} %param.15) | copy-start | bytes 393220
  7.2 72.6 %copy-start.7 = (f32[4096]{0:T(1024)S(1)}, f32[4096]{0:T(1024)}, u32[]{:S(2)}) copy-start(f32[4096]{0:T(1024)} %param.17) | copy-start | bytes 49156
  7.2 73.0 %copy-start.5 = (bf16[4096,8]{0,1:T(8,128)(2,1)S(1)}, bf16[4096,8]{0,1:T(8,128)(2,1)}, u32[]{:S(2)}) copy-start(bf16[4096,8]{0,1:T(8,128)(2,1)} %param.18) | copy-start | bytes 196612
  7.2 164.6 %all-gather.2.cloned.1.call-start = ((), (), s32[]{:S(2)}) async-start(), calls=%async_computation.3 | async-start | bytes 9191424 | tf_op jit(solution)/shard_map/all_gather | solution.py:344
  10.8 2.2 copy-start.1
  13.0 0.9 copy-start.2
  13.9 0.8 copy-start.3
  99.5 193.4 %reduce-scatter.2.cloned.1.call-start = ((), (), s32[]{:S(2)}) async-start(), calls=%async_computation.4 | async-start | bytes 8912896 | tf_op jit(solution)/shard_map/reduce_scatter | solution.py:350
  171.9 8.3 %copy-start.6 = (bf16[1024,4224]{1,0:T(8,128)(2,1)S(1)}, bf16[1024,4224]{1,0:T(8,128)(2,1)}, u32[]{:S(2)}) copy-start(bf16[1024,4224]{1,0:T(8,128)(2,1)} %all-gather.2.cloned.1.call-done) | copy-start | bytes 25952260
  171.9 8.3 %copy-start.9 = (bf16[1,4096,512]{2,1,0:T(8,128)(2,1)S(1)}, bf16[1,4096,512]{2,1,0:T(8,128)(2,1)}, u32[]{:S(2)}) copy-start(bf16[1,4096,512]{2,1,0:T(8,128)(2,1)} %param.21) | copy-start | bytes 12582916
  180.2 4.7 %copy-start.10 = (bf16[1,512,4096]{2,1,0:T(8,128)(2,1)S(1)}, bf16[1,512,4096]{2,1,0:T(8,128)(2,1)}, u32[]{:S(2)}) copy-start(bf16[1,512,4096]{2,1,0:T(8,128)(2,1)} %param.22) | copy-start | bytes 12582916
  292.9 15.2 %all-to-all-start.1 = ((bf16[8,8,4096]{2,1,0:T(8,128)(2,1)}), bf16[8,8,4096]{2,1,0:T(8,128)(2,1)S(1)}, u32[]{:S(2)}, u32[]{:S(2)}) async-start(bf16[8,8,4096]{2,1,0:T(8,128)(2,1)} %bitcast.37), calls=%async_computation.2 | async-start | bytes 1048576 | tf_op jit(solution)/shard_map/all_to_all | solution.py:356
Sparse Core Ops, SparseCore 0:
  99.6 72.1 all-gather.1
  191.8 101.1 reduce-scatter.1
